TPU v7x, 32 devices: a whole 2x2x4 slice. The times are simulated.
32 devices in a mesh: dp: 8 (over z, y), mp: 4 (over x, core).
Axes of the slice: x: 2, y: 2, z: 4, core: 2. Of those that a mesh axis runs over, the one named last changes fastest.
Arguments:
- inputs: bfloat16 [16384, 1024], P(('dp', 'mp')), may hold values from -6 to 6
- first_values: bfloat16 [16384, 8, 64], P('dp', 'mp'), may hold values from -6 to 6
- cotangent: bfloat16 [16384, 1024], P(('dp', 'mp')), may hold values from -6 to 6
- seq_lengths: int32 [32], P('dp'), may hold values from 0 to 1024, as said below
- value_owner: int32 [8], replicated, may hold values from 0 to 7, each once
- attn_norm_gain: float32 [1024], replicated, may hold values from 0.5 to 1.5
- attn_norm_bias: float32 [1024], replicated, may hold values from -3 to 3
- qkv_weight: bfloat16 [1024, 8, 5, 64], P(None, 'mp'), may hold values from -0.25 to 0.25
- qv_bias: float32 [8, 3, 64], P('mp'), may hold values from -3 to 3
- out_weight: bfloat16 [8, 2, 64, 1024], P('mp'), may hold values from -0.75 to 0.75
- out_bias: float32 [1024], replicated, may hold values from -3 to 3
- mlp_norm_gain: float32 [1024], replicated, may hold values from 0.5 to 1.5
- mlp_norm_bias: float32 [1024], replicated, may hold values from -3 to 3
- up_weight: bfloat16 [1024, 4096], P(None, 'mp'), may hold values from -0.1875 to 0.1875
- up_bias: float32 [4096], P('mp'), may hold values from -3 to 3
- down_weight: bfloat16 [4096, 1024], P('mp'), may hold values from -0.09375 to 0.09375
- down_bias: float32 [1024], replicated, may hold values from -3 to 3
Outputs:
- output: bfloat16 [16384, 1024], P(('dp', 'mp'))
- grad_inputs: bfloat16 [16384, 1024], P(('dp', 'mp'))
- grad_first_values: bfloat16 [16384, 8, 64], P('dp', 'mp')
- grad_attn_norm_gain: float32 [1024], replicated
- grad_attn_norm_bias: float32 [1024], replicated
- grad_qkv_weight: float32 [1024, 8, 5, 64], P(None, 'mp')
- grad_qv_bias: float32 [8, 3, 64], P('mp')
- grad_out_weight: float32 [8, 2, 64, 1024], P('mp')
- grad_out_bias: float32 [1024], replicated
- grad_mlp_norm_gain: float32 [1024], replicated
- grad_mlp_norm_bias: float32 [1024], replicated
- grad_up_weight: float32 [1024, 4096], P(None, 'mp')
- grad_up_bias: float32 [4096], P('mp')
- grad_down_weight: float32 [4096, 1024], P('mp')
- grad_down_bias: float32 [1024], replicated
Inputs may be any that keep to these rules, and one draw needn't show every extreme that they name: `seq_lengths`: each data group's 4 entries, in row order, are the lengths of the sequences packed into its 2048 rows: each 512 or 1024, then zeros for unused slots; they sum to 2048, and some group holds a sequence of 1024. A permutation: skip-value head p reuses the first layer's value head value_owner[p].
All inputs are finite; a program needn't handle non-finite values.
Results may differ from a plain program's by a relative error of at most 0.019.
Values may be sent and summed in bfloat16 or wider, within the bound.
A program may use at most 128 MiB of HBM per device.

v0:
```python
import jax
import jax.numpy as jnp
from jax import lax
from jax.sharding import PartitionSpec as P

SHORT = 512
EPSILON = 1e-05
MASKED = -1e30
GELU_C = 0.7978845608028654


def layer_norm(values, scale_gain, scale_bias):
    average = jnp.mean(values, axis=-1, keepdims=True)
    centered = values - average
    variance = jnp.mean(centered * centered, axis=-1, keepdims=True)
    return centered * lax.rsqrt(variance + EPSILON) * scale_gain + scale_bias


def gelu_tanh(values):
    return 0.5 * values * (1.0 + jnp.tanh(GELU_C * (values + 0.044715 * values * values * values)))


def row_starts(lengths, group_rows):
    ends = jnp.cumsum(lengths)
    begins = ends - lengths
    positions = jnp.arange(group_rows, dtype=jnp.int32)
    inside = begins[None, :] <= positions[:, None]
    return jnp.max(jnp.where(inside, begins[None, :], 0), axis=1)


def block_mask(starts, first_row, block_rows, span):
    own_rows = first_row + jnp.arange(block_rows, dtype=jnp.int32)
    key_rows = first_row - (span - block_rows) + jnp.arange(span, dtype=jnp.int32)
    begin = lax.dynamic_slice_in_dim(starts, first_row, block_rows, 0)
    return (key_rows[None, :] >= begin[:, None]) & (key_rows[None, :] <= own_rows[:, None])


def rows_product(left, right):
    return lax.dot_general(
        left, right, (((0,), (0,)), ((), ())), preferred_element_type=jnp.float32
    )


def back_product(left, weight):
    return lax.dot_general(
        left, weight, (((1,), (1,)), ((), ())), preferred_element_type=jnp.float32
    )


def padded_pair(keys, values_in, long_len):
    zero_pad = jnp.zeros((long_len,) + keys.shape[1:], keys.dtype)
    return (jnp.concatenate([zero_pad, keys], 0), jnp.concatenate([zero_pad, values_in], 0))


def attend_forward(queries, keys, values_in, starts, long_len, block_rows):
    group_rows, heads, width = queries.shape
    span = long_len + block_rows
    scale = width ** (-0.5)
    keys_pad, values_pad = padded_pair(keys, values_in, long_len)

    def one_block(block_index):
        first_row = block_index * block_rows
        query_blk = lax.dynamic_slice_in_dim(queries, first_row, block_rows, 0)
        key_blk = lax.dynamic_slice_in_dim(keys_pad, first_row, span, 0)
        value_blk = lax.dynamic_slice_in_dim(values_pad, first_row, span, 0)
        allowed = block_mask(starts, first_row, block_rows, span)
        scores = (
            jnp.einsum("qhd,khd->hqk", query_blk, key_blk, preferred_element_type=jnp.float32)
            * scale
        )
        scores = jnp.where(allowed[None], scores, MASKED)
        top_score = jnp.max(scores, axis=-1, keepdims=True)
        weights = jnp.exp(scores - top_score)
        totals = jnp.sum(weights, axis=-1, keepdims=True)
        probs = (weights / totals).astype(jnp.bfloat16)
        mixed = jnp.einsum("hqk,khd->qhd", probs, value_blk, preferred_element_type=jnp.float32)
        return (mixed.astype(jnp.bfloat16), top_score[..., 0] + jnp.log(totals[..., 0]))

    mixed, log_totals = lax.map(one_block, jnp.arange(group_rows // block_rows, dtype=jnp.int32))
    return (mixed.reshape(group_rows, heads, width), log_totals)


def attend_backward(queries, keys, values_in, grad_mixed, log_totals, starts, long_len, block_rows):
    group_rows, heads, width = queries.shape
    span = long_len + block_rows
    scale = width ** (-0.5)
    keys_pad, values_pad = padded_pair(keys, values_in, long_len)

    def one_block(carried, block_index):
        grad_keys, grad_values = carried
        first_row = block_index * block_rows
        query_blk = lax.dynamic_slice_in_dim(queries, first_row, block_rows, 0)
        key_blk = lax.dynamic_slice_in_dim(keys_pad, first_row, span, 0)
        value_blk = lax.dynamic_slice_in_dim(values_pad, first_row, span, 0)
        grad_blk = lax.dynamic_slice_in_dim(grad_mixed, first_row, block_rows, 0)
        allowed = block_mask(starts, first_row, block_rows, span)
        scores = (
            jnp.einsum("qhd,khd->hqk", query_blk, key_blk, preferred_element_type=jnp.float32)
            * scale
        )
        probs = jnp.where(allowed[None], jnp.exp(scores - log_totals[block_index][:, :, None]), 0.0)
        grad_probs = jnp.einsum(
            "qhd,khd->hqk", grad_blk, value_blk, preferred_element_type=jnp.float32
        )
        inner = jnp.sum(probs * grad_probs, axis=-1, keepdims=True)
        grad_scores = (probs * (grad_probs - inner)).astype(jnp.bfloat16)
        grad_query = (
            jnp.einsum("hqk,khd->qhd", grad_scores, key_blk, preferred_element_type=jnp.float32)
            * scale
        )
        grad_key = (
            jnp.einsum("hqk,qhd->khd", grad_scores, query_blk, preferred_element_type=jnp.float32)
            * scale
        )
        grad_value = jnp.einsum(
            "hqk,qhd->khd", probs.astype(jnp.bfloat16), grad_blk, preferred_element_type=jnp.float32
        )
        grad_keys = lax.dynamic_update_slice_in_dim(
            grad_keys,
            lax.dynamic_slice_in_dim(grad_keys, first_row, span, 0) + grad_key,
            first_row,
            0,
        )
        grad_values = lax.dynamic_update_slice_in_dim(
            grad_values,
            lax.dynamic_slice_in_dim(grad_values, first_row, span, 0) + grad_value,
            first_row,
            0,
        )
        return ((grad_keys, grad_values), grad_query)

    zero_grads = jnp.zeros((long_len + group_rows, heads, width), jnp.float32)
    (grad_keys, grad_values), grad_queries = lax.scan(
        one_block, (zero_grads, zero_grads), jnp.arange(group_rows // block_rows, dtype=jnp.int32)
    )
    return (
        grad_queries.reshape(group_rows, heads, width),
        grad_keys[long_len:],
        grad_values[long_len:],
    )


def body(
    inputs,
    first_values,
    cotangent,
    seq_lengths,
    value_owner,
    attn_norm_gain,
    attn_norm_bias,
    qkv_weight,
    qv_bias,
    out_weight,
    out_bias,
    mlp_norm_gain,
    mlp_norm_bias,
    up_weight,
    up_bias,
    down_weight,
    down_bias,
):
    local_rows = inputs.shape[0]
    model_width = inputs.shape[1]
    group_rows = local_rows * lax.axis_size("mp")
    pairs_dev = qkv_weight.shape[1]
    head_size = qkv_weight.shape[3]
    heads_dev = 2 * pairs_dev
    all_pairs = value_owner.shape[0]
    long_len = 2 * SHORT
    block_rows = min(512, group_rows)
    starts = row_starts(seq_lengths, group_rows)
    all_first = lax.all_gather(first_values, "mp", axis=1, tiled=True)
    owners = lax.dynamic_slice_in_dim(value_owner, lax.axis_index("mp") * pairs_dev, pairs_dev, 0)
    skip_values = jnp.take(all_first, owners, axis=1)
    qkv_flat = qkv_weight.reshape(model_width, pairs_dev * 5 * head_size)
    out_flat = out_weight.reshape(heads_dev * head_size, model_width)

    def run_forward(layer_in):
        inputs_f = layer_in.astype(jnp.float32)
        normed_one = layer_norm(inputs_f, attn_norm_gain, attn_norm_bias).astype(jnp.bfloat16)
        rows_one = lax.all_gather(normed_one, "mp", axis=0, tiled=True)
        projected = jnp.dot(rows_one, qkv_flat, preferred_element_type=jnp.float32)
        projected = projected.reshape(group_rows, pairs_dev, 5, head_size)
        queries = (projected[:, :, 0:2] + qv_bias[None, :, 0:2]).astype(jnp.bfloat16)
        queries = queries.reshape(group_rows, heads_dev, head_size)
        keys = projected[:, :, 2:4].astype(jnp.bfloat16).reshape(group_rows, heads_dev, head_size)
        fresh = (projected[:, :, 4] + qv_bias[None, :, 2]).astype(jnp.bfloat16)
        values_all = jnp.stack([fresh, skip_values], axis=2).reshape(
            group_rows, heads_dev, head_size
        )
        mixed, log_totals = attend_forward(queries, keys, values_all, starts, long_len, block_rows)
        mixed_flat = mixed.reshape(group_rows, heads_dev * head_size)
        picked = mixed_flat
        residual = (
            inputs_f
            + lax.psum_scatter(
                jnp.dot(picked, out_flat, preferred_element_type=jnp.float32).astype(jnp.bfloat16),
                "mp",
                scatter_dimension=0,
                tiled=True,
            ).astype(jnp.float32)
            + out_bias
        )
        normed_two = layer_norm(residual, mlp_norm_gain, mlp_norm_bias).astype(jnp.bfloat16)
        rows_two = lax.all_gather(normed_two, "mp", axis=0, tiled=True)
        hidden_pre = jnp.dot(rows_two, up_weight, preferred_element_type=jnp.float32) + up_bias
        hidden = gelu_tanh(hidden_pre).astype(jnp.bfloat16)
        picked = hidden
        layer_out = (
            residual
            + lax.psum_scatter(
                jnp.dot(picked, down_weight, preferred_element_type=jnp.float32).astype(
                    jnp.bfloat16
                ),
                "mp",
                scatter_dimension=0,
                tiled=True,
            ).astype(jnp.float32)
            + down_bias
        )
        return (
            layer_out,
            inputs_f,
            residual,
            rows_one,
            queries,
            keys,
            values_all,
            log_totals,
            mixed_flat,
            rows_two,
            hidden_pre,
            hidden,
        )

    saved = run_forward(inputs)
    output = saved[0].astype(jnp.bfloat16)
    again_in = lax.optimization_barrier((inputs, saved[0]))[0]
    saved = run_forward(again_in)
    (
        inputs_f,
        residual,
        rows_one,
        queries,
        keys,
        values_all,
        log_totals,
        mixed_flat,
        rows_two,
        hidden_pre,
        hidden,
    ) = saved[1:]
    grad_out_f = cotangent.astype(jnp.float32)
    grad_rows = lax.all_gather(cotangent, "mp", axis=0, tiled=True)
    grad_hidden = back_product(grad_rows, down_weight)
    gelu_pair = jax.vjp(gelu_tanh, hidden_pre)
    grad_pre = gelu_pair[1](grad_hidden)[0].astype(jnp.bfloat16)
    grad_down_weight = rows_product(hidden, grad_rows)
    grad_up_weight = rows_product(rows_two, grad_pre)
    grad_up_bias = jnp.sum(grad_pre.astype(jnp.float32), axis=0)
    grad_down_bias = jnp.sum(grad_out_f, axis=0)
    grad_normed_two = lax.psum_scatter(
        back_product(grad_pre, up_weight).astype(jnp.bfloat16),
        "mp",
        scatter_dimension=0,
        tiled=True,
    ).astype(jnp.float32)
    norm_two_pair = jax.vjp(layer_norm, residual, mlp_norm_gain, mlp_norm_bias)
    grad_through, grad_mlp_norm_gain, grad_mlp_norm_bias = norm_two_pair[1](grad_normed_two)
    grad_residual = grad_out_f + grad_through
    grad_out_bias = jnp.sum(grad_residual, axis=0)
    resid_rows = lax.all_gather(grad_residual.astype(jnp.bfloat16), "mp", axis=0, tiled=True)
    grad_out_weight = rows_product(mixed_flat, resid_rows).reshape(out_weight.shape)
    grad_mixed = back_product(resid_rows, out_flat).astype(jnp.bfloat16)
    grad_mixed = grad_mixed.reshape(group_rows, heads_dev, head_size)
    grad_query, grad_key, grad_value = attend_backward(
        queries, keys, values_all, grad_mixed, log_totals, starts, long_len, block_rows
    )
    grad_value = grad_value.reshape(group_rows, pairs_dev, 2, head_size)
    grad_projected = jnp.concatenate(
        [
            grad_query.reshape(group_rows, pairs_dev, 2, head_size),
            grad_key.reshape(group_rows, pairs_dev, 2, head_size),
            grad_value[:, :, 0:1],
        ],
        axis=2,
    ).astype(jnp.bfloat16)
    grad_qv_bias = jnp.concatenate(
        [
            jnp.sum(grad_projected[:, :, 0:2].astype(jnp.float32), axis=0),
            jnp.sum(grad_projected[:, :, 4:5].astype(jnp.float32), axis=0),
        ],
        axis=1,
    )
    grad_flat = grad_projected.reshape(group_rows, pairs_dev * 5 * head_size)
    grad_qkv_weight = rows_product(rows_one, grad_flat).reshape(qkv_weight.shape)
    grad_normed_one = lax.psum_scatter(
        back_product(grad_flat, qkv_flat).astype(jnp.bfloat16),
        "mp",
        scatter_dimension=0,
        tiled=True,
    ).astype(jnp.float32)
    norm_one_pair = jax.vjp(layer_norm, inputs_f, attn_norm_gain, attn_norm_bias)
    grad_through_one, grad_attn_norm_gain, grad_attn_norm_bias = norm_one_pair[1](grad_normed_one)
    grad_inputs = (grad_residual + grad_through_one).astype(jnp.bfloat16)
    every_skip = lax.all_gather(grad_value[:, :, 1].astype(jnp.bfloat16), "mp", axis=1, tiled=True)
    owned = lax.axis_index("mp") * pairs_dev + jnp.arange(pairs_dev, dtype=jnp.int32)
    every_pair = jnp.arange(all_pairs, dtype=jnp.int32)
    inverse = jnp.sum(
        jnp.where(value_owner[None, :] == owned[:, None], every_pair[None, :], 0), axis=1
    )
    grad_first = jnp.take(every_skip, inverse, axis=1)
    weight_sums = (
        lax.psum(grad_qkv_weight.astype(jnp.bfloat16), "dp").astype(jnp.float32),
        lax.psum(grad_qv_bias.astype(jnp.bfloat16), "dp").astype(jnp.float32),
        lax.psum(grad_out_weight.astype(jnp.bfloat16), "dp").astype(jnp.float32),
        lax.psum(grad_up_weight.astype(jnp.bfloat16), "dp").astype(jnp.float32),
        lax.psum(grad_up_bias.astype(jnp.bfloat16), "dp").astype(jnp.float32),
        lax.psum(grad_down_weight.astype(jnp.bfloat16), "dp").astype(jnp.float32),
    )
    norm_sums = lax.psum(
        (
            grad_attn_norm_gain,
            grad_attn_norm_bias,
            grad_out_bias,
            grad_mlp_norm_gain,
            grad_mlp_norm_bias,
            grad_down_bias,
        ),
        ("dp", "mp"),
    )
    return (
        output,
        grad_inputs,
        grad_first,
        norm_sums[0],
        norm_sums[1],
        weight_sums[0],
        weight_sums[1],
        weight_sums[2],
        norm_sums[2],
        norm_sums[3],
        norm_sums[4],
        weight_sums[3],
        weight_sums[4],
        weight_sums[5],
        norm_sums[5],
    )


def solution(mesh):
    return jax.shard_map(
        body,
        mesh=mesh,
        in_specs=(
            P(("dp", "mp"), None),
            P("dp", "mp", None),
            P(("dp", "mp"), None),
            P("dp"),
            P(),
            P(),
            P(),
            P(None, "mp", None, None),
            P("mp", None, None),
            P("mp", None, None, None),
            P(),
            P(),
            P(),
            P(None, "mp"),
            P("mp"),
            P("mp", None),
            P(),
        ),
        out_specs=(
            P(("dp", "mp"), None),
            P(("dp", "mp"), None),
            P("dp", "mp", None),
            P(),
            P(),
            P(None, "mp", None, None),
            P("mp", None, None),
            P("mp", None, None, None),
            P(),
            P(),
            P(),
            P(None, "mp"),
            P("mp"),
            P("mp", None),
            P(),
        ),
        check_vma=False,
    )
```

profile of v0, /device:TPU:0, one launch (start us, length us, event | category | flops | bytes accessed | tf_op | source)
XLA Modules:
  0.0 1232.0 jit_solution(12711491678477917356)
XLA Ops:
  13.3 21.6 %all-gather.12.cloned.1.call-done = bf16[2048,8,64]{0,2,1:T(8,128)(2,1)} async-done(((bf16[2048,2,64]{0,2,1:T(8,128)(2,1)}), bf16[2048,8,64]{0,2,1:T(8,128)(2,1)}) %all-gather.12.cloned.1.call-update) | async-done | bytes 2097168 | tf_op jit(solution)/shard_map/all_gather | solution.py:172
  38.0 33.5 %all-gather.10.cloned.1.call-done = bf16[2048,1024]{1,0:T(8,128)(2,1)} async-done(((bf16[512,1024]{1,0:T(8,128)(2,1)}), bf16[2048,1024]{1,0:T(8,128)(2,1)}) %all-gather.10.cloned.1.call-update) | async-done | bytes 4194320 | tf_op jit(solution)/shard_map/all_gather | solution.py:181
  81.7 132.5 %while.42 = (s32[]{:T(128)}, bf16[4,512,4,64]{1,3,2,0:T(8,128)(2,1)}, s32[4]{0:T(128)S(1)}, bf16[3072,4,64]{0,2,1:T(8,128)(2,1)}, s32[2048]{0:T(1024)S(1)}, /*in...) while((s32[]{:T(128)}, ...), condition=%wide.region_7.9_spmd, body=%wide.region_4.8_spmd.sunk | while | flops 832966144 | bytes 60332316 | solution.py:79
  91.2 16.2 %fusion.196 = (f32[4,512]{1,0:T(4,128)S(1)}, f32[4,512,1536]{2,1,0:T(8,128)}) fusion(f32[4,512,1536]{2,1,0:T(8,128)} %fusion.195, pred[512,1536]{1,0:T(8,128)(4,1)S(1)} %compare_and_fusion.8), kind=kOutput, calls=%fused_computation.224.clone.1 | output fusion | flops 18875904 | bytes 25960448 | tf_op jit(solution)/shard_map/while/body/eval_jaxpr/sub | solution.py:73
  124.4 16.2 %fusion.196 = (f32[4,512]{1,0:T(4,128)S(1)}, f32[4,512,1536]{2,1,0:T(8,128)}) fusion(f32[4,512,1536]{2,1,0:T(8,128)} %fusion.195, pred[512,1536]{1,0:T(8,128)(4,1)S(1)} %compare_and_fusion.8), kind=kOutput, calls=%fused_computation.224.clone.1 | output fusion | flops 18875904 | bytes 25960448 | tf_op jit(solution)/shard_map/while/body/eval_jaxpr/sub | solution.py:73
  157.5 16.2 %fusion.196 = (f32[4,512]{1,0:T(4,128)S(1)}, f32[4,512,1536]{2,1,0:T(8,128)}) fusion(f32[4,512,1536]{2,1,0:T(8,128)} %fusion.195, pred[512,1536]{1,0:T(8,128)(4,1)S(1)} %compare_and_fusion.8), kind=kOutput, calls=%fused_computation.224.clone.1 | output fusion | flops 18875904 | bytes 25960448 | tf_op jit(solution)/shard_map/while/body/eval_jaxpr/sub | solution.py:73
  190.6 16.2 %fusion.196 = (f32[4,512]{1,0:T(4,128)S(1)}, f32[4,512,1536]{2,1,0:T(8,128)}) fusion(f32[4,512,1536]{2,1,0:T(8,128)} %fusion.195, pred[512,1536]{1,0:T(8,128)(4,1)S(1)} %compare_and_fusion.8), kind=kOutput, calls=%fused_computation.224.clone.1 | output fusion | flops 18875904 | bytes 25960448 | tf_op jit(solution)/shard_map/while/body/eval_jaxpr/sub | solution.py:73
  220.2 44.5 %reduce-scatter.6.cloned.1.call-done = bf16[512,1024]{1,0:T(8,128)(2,1)} async-done(((bf16[2048,1024]{1,0:T(8,128)(2,1)}), bf16[512,1024]{1,0:T(8,128)(2,1)}) %reduce-scatter.6.cloned.1.call-update) | async-done | bytes 1048592 | tf_op jit(solution)/shard_map/reduce_scatter | solution.py:196
  268.6 34.6 %all-gather.14.cloned.1.call-done = bf16[2048,1024]{1,0:T(8,128)(2,1)} async-done(((bf16[512,1024]{1,0:T(8,128)(2,1)}), bf16[2048,1024]{1,0:T(8,128)(2,1)}) %all-gather.14.cloned.1.call-update) | async-done | bytes 4194320 | tf_op jit(solution)/shard_map/all_gather | solution.py:205
  303.2 12.9 %fusion.81 = bf16[2048,1024]{1,0:T(8,128)(2,1)} fusion(bf16[1024,1024]{1,0:T(8,128)(2,1)} %param.40, f32[1024]{0:T(1024)S(1)} %copy-done.60, bf16[2048,1024]{1,0:T(8,128)(2,1)} %all-gather.14.cloned.1.call-done, bf16[1024,1024]{1,0:T(8,128)(2,1)S(1)} %copy-done), kind=kOutput, calls=%fused_computation.106 | convolution fusion | flops 8613003264 | bytes 12587008 | tf_op jit(solution)/shard_map/dot_general | solution.py:212
  316.2 44.7 %reduce-scatter.8.cloned.1.call-done = bf16[512,1024]{1,0:T(8,128)(2,1)} async-done(((bf16[2048,1024]{1,0:T(8,128)(2,1)}), bf16[512,1024]{1,0:T(8,128)(2,1)}) %reduce-scatter.8.cloned.1.call-update) | async-done | bytes 1048592 | tf_op jit(solution)/shard_map/reduce_scatter | solution.py:211
  367.6 34.3 %all-gather.16.cloned.1.call-done = bf16[2048,1024]{1,0:T(8,128)(2,1)} async-done(((bf16[512,1024]{1,0:T(8,128)(2,1)}), bf16[2048,1024]{1,0:T(8,128)(2,1)}) %all-gather.16.cloned.1.call-update) | async-done | bytes 4194320 | tf_op jit(solution)/shard_map/all_gather | solution.py:181
  412.4 55.7 %while.43 = (s32[]{:T(128)}, bf16[4,512,4,64]{1,3,2,0:T(8,128)(2,1)}, f32[4,4,512]{2,1,0:T(4,128)S(1)}, s32[4]{0:T(128)S(1)}, bf16[3072,4,64]{0,2,1:T(8,128)(2,1...) while((s32[]{:T(128)}, ...), condition=%wide.region_17.19_spmd, body=%wide.region_14.18_spmd.sunk | while | flops 845545472 | bytes 49371432 | solution.py:79
  475.3 44.2 %reduce-scatter.10.cloned.1.call-done = bf16[512,1024]{1,0:T(8,128)(2,1)} async-done(((bf16[2048,1024]{1,0:T(8,128)(2,1)}), bf16[512,1024]{1,0:T(8,128)(2,1)}) %reduce-scatter.10.cloned.1.call-update) | async-done | bytes 1048592 | tf_op jit(solution)/shard_map/reduce_scatter | solution.py:196
  524.3 33.8 %all-gather.18.cloned.1.call-done = bf16[2048,1024]{1,0:T(8,128)(2,1)} async-done(((bf16[512,1024]{1,0:T(8,128)(2,1)}), bf16[2048,1024]{1,0:T(8,128)(2,1)}) %all-gather.18.cloned.1.call-update) | async-done | bytes 4194320 | tf_op jit(solution)/shard_map/all_gather | solution.py:205
  558.1 9.0 fusion.146
  567.1 27.1 %all-gather.20.cloned.1.call-done = bf16[2048,1024]{1,0:T(8,128)(2,1)} async-done(((bf16[512,1024]{1,0:T(8,128)(2,1)}), bf16[2048,1024]{1,0:T(8,128)(2,1)}) %all-gather.20.cloned.1.call-update) | async-done | bytes 4194320 | tf_op jit(solution)/shard_map/all_gather | solution.py:254
  594.2 15.5 %fusion.141 = (bf16[1024]{0:T(1024)(128)(2,1)}, bf16[2048,1024]{1,0:T(8,128)(2,1)S(1)}) fusion(f32[2048,1024]{1,0:T(8,128)} %fusion.146, f32[1024]{0:T(1024)S(1)} %copy-done.61, bf16[2048,1024]{1,0:T(8,128)(2,1)} %all-gather.20.cloned.1.call-done, bf16[1024,1024]{1,0:T(8,128)(2,1)} %param.40), kind=kOutput, calls=%fused_computation.222 | convolution fusion | flops 4349492224 | bytes 18880512 | tf_op jit(solution)/shard_map/dot_general | solution.py:45
  618.1 44.5 %reduce-scatter.12.cloned.1.call-done = bf16[512,1024]{1,0:T(8,128)(2,1)} async-done(((bf16[2048,1024]{1,0:T(8,128)(2,1)}), bf16[512,1024]{1,0:T(8,128)(2,1)}) %reduce-scatter.12.cloned.1.call-update) | async-done | bytes 1048592 | tf_op jit(solution)/shard_map/reduce_scatter | solution.py:262
  672.0 9.5 convolution_convert_fusion.4
  681.5 25.1 %all-gather.22.cloned.1.call-done = bf16[2048,1024]{1,0:T(8,128)(2,1)} async-done(((bf16[512,1024]{1,0:T(8,128)(2,1)}), bf16[2048,1024]{1,0:T(8,128)(2,1)}) %all-gather.22.cloned.1.call-update) | async-done | bytes 4194320 | tf_op jit(solution)/shard_map/all_gather | solution.py:272
  715.1 180.7 %while.44 = (s32[]{:T(128)}, f32[3072,4,64]{0,2,1:T(8,128)}, f32[3072,4,64]{0,2,1:T(8,128)}, bf16[4,512,4,64]{1,0,3,2:T(4,128)(2,1)}, s32[4]{0:T(128)S(1)}, /*in...) while((s32[]{:T(128)}, f32[3072,4,64]{0,2,1:T(8,128)}, ...), condition=%wide.region_26.28_spmd, body=%wide.region_24.27_spmd.sunk | while | flops 2045378560 | bytes 163641856 | solution.py:133
  750.1 10.3 dynamic_update_slice.55
  767.6 8.5 multiply_reduce_fusion.4
  795.3 10.3 dynamic_update_slice.55
  840.4 10.3 dynamic_update_slice.55
  885.5 10.3 dynamic_update_slice.55
  899.0 11.9 fusion.110
  935.6 22.7 %all-reduce.5 = (bf16[2,3,64]{2,1,0:T(4,128)(2,1)S(1)}, bf16[1024]{0:T(1024)(128)(2,1)S(1)}) all-reduce(bf16[2,3,64]{2,1,0:T(4,128)(2,1)S(1)} %pad_maximum_fusion.2, bf16[1024]{0:T(1024)(128)(2,1)S(1)} %copy-done.54), channel_id=1, replica_groups=mesh['dp'=8,'mp'=4] {'dp'}, use_global_device_ids=true, to_apply=%region_38.40 | all-reduce | flops 1408 | bytes 5632 | tf_op jit(solution)/shard_map/psum | solution.py:315
  962.6 169.5 %all-reduce.9.cloned.1.call-done = (bf16[1024,2,5,64]{0,3,2,1:T(8,128)(2,1)}, bf16[2,2,64,1024]{3,2,1,0:T(8,128)(2,1)}, bf16[1024,1024]{1,0:T(8,128)(2,1)}, bf16[1024,1024]{1,0:T(8,128)(2,1)}) async-done(((bf16[1024,2,5,64]{0,3,2,1:T(8,128)(2,1)}, bf16[2,2,64,1024]{3,2,1,0:T(8,128)(2,1)}, bf16[1024,1024]{1,0:T(8,128)(2,1)}, bf16[1024,1024]{1,0:T(8,128)(2,1)}), (bf16[1024,2,5,64]{0,3,2,1:T(8,128)(2,1)}, ...) | async-done | bytes 6029328 | tf_op jit(solution)/shard_map/psum | solution.py:314
  1143.0 35.2 %reduce-scatter.14.cloned.1.call-done = bf16[512,1024]{1,0:T(8,128)(2,1)} async-done(((bf16[2048,1024]{1,0:T(8,128)(2,1)}), bf16[512,1024]{1,0:T(8,128)(2,1)}) %reduce-scatter.14.cloned.1.call-update) | async-done | bytes 1048592 | tf_op jit(solution)/shard_map/reduce_scatter | solution.py:297
  1181.4 39.9 %all-reduce.4 = (f32[1024]{0:T(1024)}, f32[1024]{0:T(1024)}, f32[1024]{0:T(1024)}, f32[1024]{0:T(1024)}, f32[1024]{0:T(1024)}, /*index=5*/f32[1024]{0:T(1024)}) all-reduce(f32[1024]{0:T(1024)S(1)} %get-tuple-element.386, f32[1024]{0:T(1024)S(1)} %get-tuple-element.390, ...), channel_id=1, replica_groups=mesh['dp'=8,'mp'=4] {'dp','mp'}, use_global_device_ids=true, to_apply=%region_32.34 | all-reduce | flops 6144 | bytes 49152 | tf_op jit(solution)/shard_map/psum | solution.py:321
  (415 shorter events, 371.9 us)
Async XLA Ops:
  7.2 296.0 %copy-start = (bf16[1024,1024]{1,0:T(8,128)(2,1)S(1)}, bf16[1024,1024]{1,0:T(8,128)(2,1)}, u32[]{:S(2)}) copy-start(bf16[1024,1024]{1,0:T(8,128)(2,1)} %param.38) | copy-start | bytes 6291460
  7.2 27.7 %all-gather.12.cloned.1.call-start = ((), (), s32[]{:S(2)}) async-start(), calls=%async_computation.6 | async-start | bytes 2621440 | tf_op jit(solution)/shard_map/all_gather | solution.py:172
  8.0 63.5 %all-gather.10.cloned.1.call-start = ((), (), s32[]{:S(2)}) async-start(), calls=%async_computation.5 | async-start | bytes 5242880 | tf_op jit(solution)/shard_map/all_gather | solution.py:181
  12.8 251.8 %reduce-scatter.6.cloned.1.call-start = ((), (), s32[]{:S(2)}) async-start(), calls=%async_computation.7 | async-start | bytes 5242880 | tf_op jit(solution)/shard_map/reduce_scatter | solution.py:196
  13.0 63.9 %copy-start.40 = (f32[2,2,64]{2,1,0:T(2,128)}, f32[2,2,64]{2,1,0:T(2,128)S(1)}, u32[]{:S(2)}) copy-start(f32[2,2,64]{2,1,0:T(2,128)S(1)} %copy.44) | copy-start | bytes 3076
  13.3 63.5 %copy-start.50 = (f32[2,64]{1,0:T(2,128)}, f32[2,64]{1,0:T(2,128)S(1)}, u32[]{:S(2)}) copy-start(f32[2,64]{1,0:T(2,128)S(1)} %slice_bitcast_fusion) | copy-start | bytes 1540
  219.9 44.8 %copy-start.2 = (bf16[512,1024]{1,0:T(8,128)(2,1)S(1)}, bf16[512,1024]{1,0:T(8,128)(2,1)}, u32[]{:S(2)}) copy-start(bf16[512,1024]{1,0:T(8,128)(2,1)} %param.25) | copy-start | bytes 3145732
  219.9 44.8 %copy-start.28 = (f32[1024]{0:T(1024)S(1)}, f32[1024]{0:T(1024)}, u32[]{:S(2)}) copy-start(f32[1024]{0:T(1024)} %param.35) | copy-start | bytes 12292
  219.9 47.1 %copy-start.29 = (f32[1024]{0:T(1024)S(1)}, f32[1024]{0:T(1024)}, u32[]{:S(2)}) copy-start(f32[1024]{0:T(1024)} %param.36) | copy-start | bytes 12292
  219.9 47.1 %copy-start.44 = (f32[1024]{0:T(1024)S(1)}, f32[1024]{0:T(1024)}, u32[]{:S(2)}) copy-start(f32[1024]{0:T(1024)} %param.37) | copy-start | bytes 12292
  219.9 83.3 %all-gather.14.cloned.1.call-start = ((), (), s32[]{:S(2)}) async-start(), calls=%async_computation.8 | async-start | bytes 5242880 | tf_op jit(solution)/shard_map/all_gather | solution.py:205
  268.6 92.3 %reduce-scatter.8.cloned.1.call-start = ((), (), s32[]{:S(2)}) async-start(), calls=%async_computation.9 | async-start | bytes 5242880 | tf_op jit(solution)/shard_map/reduce_scatter | solution.py:211
  316.1 44.8 %copy-start.53 = (f32[1024]{0:T(1024)S(1)}, f32[1024]{0:T(1024)}, u32[]{:S(2)}) copy-start(f32[1024]{0:T(1024)} %param.41) | copy-start | bytes 12292
  316.2 49.7 %copy-start.32 = (f32[1024]{0:T(1024)S(1)}, f32[1024]{0:T(1024)}, u32[]{:S(2)}) copy-start(f32[1024]{0:T(1024)} %param.30) | copy-start | bytes 12292
  316.2 49.7 %copy-start.43 = (f32[1024]{0:T(1024)S(1)}, f32[1024]{0:T(1024)}, u32[]{:S(2)}) copy-start(f32[1024]{0:T(1024)} %param.31) | copy-start | bytes 12292
  316.2 85.8 %all-gather.16.cloned.1.call-start = ((), (), s32[]{:S(2)}) async-start(), calls=%async_computation.10 | async-start | bytes 5242880 | tf_op jit(solution)/shard_map/all_gather | solution.py:181
  367.3 152.2 %reduce-scatter.10.cloned.1.call-start = ((), (), s32[]{:S(2)}) async-start(), calls=%async_computation.11 | async-start | bytes 5242880 | tf_op jit(solution)/shard_map/reduce_scatter | solution.py:196
  367.6 39.4 %copy-start.51 = (f32[2,64]{1,0:T(2,128)S(1)}, f32[2,64]{1,0:T(2,128)}, u32[]{:S(2)}) copy-start(f32[2,64]{1,0:T(2,128)} %copy-done.50) | copy-start | bytes 1540
  367.6 39.6 %copy-start.41 = (f32[2,2,64]{2,1,0:T(2,128)S(1)}, f32[2,2,64]{2,1,0:T(2,128)}, u32[]{:S(2)}) copy-start(f32[2,2,64]{2,1,0:T(2,128)} %copy-done.40) | copy-start | bytes 3076
  474.8 47.1 %copy-start.30 = (f32[1024]{0:T(1024)S(1)}, f32[1024]{0:T(1024)}, u32[]{:S(2)}) copy-start(f32[1024]{0:T(1024)} %param.36) | copy-start | bytes 12292
  474.8 47.0 %copy-start.45 = (f32[1024]{0:T(1024)S(1)}, f32[1024]{0:T(1024)}, u32[]{:S(2)}) copy-start(f32[1024]{0:T(1024)} %param.37) | copy-start | bytes 12292
  474.8 83.3 %all-gather.18.cloned.1.call-start = ((), (), s32[]{:S(2)}) async-start(), calls=%async_computation.12 | async-start | bytes 5242880 | tf_op jit(solution)/shard_map/all_gather | solution.py:205
  523.5 70.7 %all-gather.20.cloned.1.call-start = ((), (), s32[]{:S(2)}) async-start(), calls=%async_computation.13 | async-start | bytes 5242880 | tf_op jit(solution)/shard_map/all_gather | solution.py:254
  524.2 70.0 %copy-start.61 = (f32[1024]{0:T(1024)S(1)}, f32[1024]{0:T(1024)}, u32[]{:S(2)}) copy-start(f32[1024]{0:T(1024)} %param.39) | copy-start | bytes 12292
  524.2 138.5 %reduce-scatter.12.cloned.1.call-start = ((), (), s32[]{:S(2)}) async-start(), calls=%async_computation.14 | async-start | bytes 5242880 | tf_op jit(solution)/shard_map/reduce_scatter | solution.py:262
  617.9 88.7 %all-gather.22.cloned.1.call-start = ((), (), s32[]{:S(2)}) async-start(), calls=%async_computation.15 | async-start | bytes 5242880 | tf_op jit(solution)/shard_map/all_gather | solution.py:272
  672.0 287.5 %all-gather.24.cloned.1.call-start = ((), (), s32[]{:S(2)}) async-start(), calls=%async_computation.17 | async-start | bytes 2621440 | tf_op jit(solution)/shard_map/all_gather | solution.py:306
  898.7 233.4 %all-reduce.9.cloned.1.call-start = ((), (), s32[]{:S(2)}) async-start(), calls=%async_computation.18 | async-start | bytes 12058624 | tf_op jit(solution)/shard_map/psum | solution.py:314
  923.9 254.2 %reduce-scatter.14.cloned.1.call-start = ((), (), s32[]{:S(2)}) async-start(), calls=%async_computation.16 | async-start | bytes 5242880 | tf_op jit(solution)/shard_map/reduce_scatter | solution.py:297
  1140.0 40.1 %copy-start.39 = (f32[512]{0:T(512)S(1)}, f32[512]{0:T(512)}, u32[]{:S(2)}) copy-start(f32[512]{0:T(512)} %copy-done.38) | copy-start | bytes 6148
  1140.0 40.2 %copy-start.37 = (f32[512]{0:T(512)S(1)}, f32[512]{0:T(512)}, u32[]{:S(2)}) copy-start(f32[512]{0:T(512)} %copy-done.36) | copy-start | bytes 6148
  1142.9 38.5 %copy-start.49 = (f32[1024]{0:T(1024)S(1)}, f32[1024]{0:T(1024)}, u32[]{:S(2)}) copy-start(f32[1024]{0:T(1024)} %get-tuple-element.468) | copy-start | bytes 12292
  (69 other events, 533.3 us)
Sparse Core Ops, SparseCore 0:
  9.6 25.2 all-gather.11
  37.0 34.4 all-gather.9
  220.0 44.5 reduce-scatter.5
  268.7 34.4 all-gather.13
  316.3 44.5 reduce-scatter.7
  367.5 34.4 all-gather.15
  474.9 44.5 reduce-scatter.9
  523.6 34.4 all-gather.17
  559.7 34.4 all-gather.19
  618.0 44.5 reduce-scatter.11
  672.1 34.4 all-gather.21
  898.8 22.5 all-gather.23
  927.2 204.8 all-reduce.8
  1134.5 43.6 reduce-scatter.13
where the time goes:
time: 1250 us; the launch traced here: 1230 us
  waiting for transfers between devices  594 us (48%)
  matrix products  280 us (22%)
  other arithmetic  162 us (13%)
  local copies, waits for them, and re-layouts  99.3 us (8%)
  blocking collectives  62.6 us (5%)
  loops' own time  16.5 us (1%)
  between operations  15.2 us (1%)
    psum x1, waiting for transfers between devices, body(): lax.psum(grad_qkv_weight.astype(jnp.bfloat16), 'dp').astype(jnp.float32)  170 us
    reduce_scatter x2, waiting for transfers between devices, run_forward(): lax.psum_scatter(jnp.dot(picked, out_flat, preferred_element_type=jnp.flo...  88.7 us
    dot_general x12, matrix products, one_block(): jnp.einsum('qhd,khd->hqk', query_blk, key_blk, preferred_element_type=jnp...  78.7 us
    all_gather x2, waiting for transfers between devices, run_forward(): rows_two = lax.all_gather(normed_two, 'mp', axis=0, tiled=True)  68.4 us
    all_gather x2, waiting for transfers between devices, run_forward(): rows_one = lax.all_gather(normed_one, 'mp', axis=0, tiled=True)  67.9 us
    sub x4, other arithmetic, one_block(): weights = jnp.exp(scores - top_score)  64.7 us
    dot_general x8, matrix products, one_block(): jnp.einsum('hqk,khd->qhd', probs, value_blk, preferred_element_type=jnp.f...  47.8 us
    reduce_scatter x1, waiting for transfers between devices, run_forward(): lax.psum_scatter(jnp.dot(picked, down_weight, preferred_element_type=jnp....  44.7 us
  transfers between devices with their start and end apart: 14, of which 13 were waited for; matrix products, arithmetic and copies ran while one was open for 6% of the time, Pallas kernels for 0%

commit v1 on v0

--- a/solution.py
+++ b/solution.py
@@ -311,7 +311,9 @@
     )
     grad_first = jnp.take(every_skip, inverse, axis=1)
     weight_sums = (
-        lax.psum(grad_qkv_weight.astype(jnp.bfloat16), "dp").astype(jnp.float32),
+        jnp.sum(lax.all_gather(grad_qkv_weight.astype(jnp.bfloat16), "dp"), axis=0).astype(
+            jnp.float32
+        ),
         lax.psum(grad_qv_bias.astype(jnp.bfloat16), "dp").astype(jnp.float32),
         lax.psum(grad_out_weight.astype(jnp.bfloat16), "dp").astype(jnp.float32),
         lax.psum(grad_up_weight.astype(jnp.bfloat16), "dp").astype(jnp.float32),

time: 1250 us -> 1310 us (1.048)
  waiting for transfers between devices: 594 us -> 667 us
    all_gather x0 -> x1, waiting for transfers between devices: none -> 102 us  [body(): lax.all_gather(grad_qkv_weight.astype(jnp.bfloat16), 'dp')]
    psum x1, waiting for transfers between devices: 170 us -> 130 us  [body(): lax.psum(grad_out_weight.astype(jnp.bfloat16), 'dp').astype(jnp.float32)]
    dynamic_update_slice x8, local copies, waits for them, and re-layouts: 42.8 us -> 19.9 us  [attend_backward(): lax.scan(one_block, (zero_grads, zero_grads), jnp.arange(group_rows // bl...]
    unnamed x119 -> x120, local copies, waits for them, and re-layouts: 11 us -> 29.5 us
  transfers between devices with their start and end apart: 14 -> 15, of which waited for: 13 -> 14; matrix products, arithmetic and copies ran while one was open for 6% -> 6% of each run, Pallas kernels for 0% -> 0%
where the time goes in v1:
time: 1310 us; the launch traced here: 1290 us
  waiting for transfers between devices  667 us (51%)
  matrix products  271 us (21%)
  other arithmetic  168 us (13%)
  local copies, waits for them, and re-layouts  87.8 us (7%)
  blocking collectives  66.9 us (5%)
  loops' own time  16.1 us (1%)
  between operations  15 us (1%)
    psum x1, waiting for transfers between devices, body(): lax.psum(grad_out_weight.astype(jnp.bfloat16), 'dp').astype(jnp.float32)  130 us
    all_gather x1, waiting for transfers between devices, body(): lax.all_gather(grad_qkv_weight.astype(jnp.bfloat16), 'dp')  102 us
    reduce_scatter x2, waiting for transfers between devices, run_forward(): lax.psum_scatter(jnp.dot(picked, out_flat, preferred_element_type=jnp.flo...  88.4 us
    all_gather x2, waiting for transfers between devices, run_forward(): rows_two = lax.all_gather(normed_two, 'mp', axis=0, tiled=True)  68.4 us
    all_gather x2, waiting for transfers between devices, run_forward(): rows_one = lax.all_gather(normed_one, 'mp', axis=0, tiled=True)  67.9 us
    dot_general x12, matrix products, one_block(): jnp.einsum('qhd,khd->hqk', query_blk, key_blk, preferred_element_type=jnp...  67.8 us
    sub x4, other arithmetic, one_block(): weights = jnp.exp(scores - top_score)  64.4 us
    dot_general x8, matrix products, one_block(): jnp.einsum('hqk,khd->qhd', probs, value_blk, preferred_element_type=jnp.f...  52.1 us
  transfers between devices with their start and end apart: 15, of which 14 were waited for; matrix products, arithmetic and copies ran while one was open for 6% of the time, Pallas kernels for 0%

profile of v1, /device:TPU:0, one launch (start us, length us, event | category | flops | bytes accessed | tf_op | source)
XLA Modules:
  0.0 1294.7 jit_solution(9222581053327956073)
XLA Ops:
  13.3 21.6 %all-gather.14.cloned.1.call-done = bf16[2048,8,64]{0,2,1:T(8,128)(2,1)} async-done(((bf16[2048,2,64]{0,2,1:T(8,128)(2,1)}), bf16[2048,8,64]{0,2,1:T(8,128)(2,1)}) %all-gather.14.cloned.1.call-update) | async-done | bytes 2097168 | tf_op jit(solution)/shard_map/all_gather | solution.py:172
  38.0 33.5 %all-gather.12.cloned.1.call-done = bf16[2048,1024]{1,0:T(8,128)(2,1)} async-done(((bf16[512,1024]{1,0:T(8,128)(2,1)}), bf16[2048,1024]{1,0:T(8,128)(2,1)}) %all-gather.12.cloned.1.call-update) | async-done | bytes 4194320 | tf_op jit(solution)/shard_map/all_gather | solution.py:181
  81.7 132.2 %while.42 = (s32[]{:T(128)}, bf16[4,512,4,64]{1,3,2,0:T(8,128)(2,1)}, s32[4]{0:T(128)S(1)}, bf16[3072,4,64]{0,2,1:T(8,128)(2,1)}, s32[2048]{0:T(1024)S(1)}, /*in...) while((s32[]{:T(128)}, ...), condition=%wide.region_7.9_spmd, body=%wide.region_4.8_spmd.sunk | while | flops 832966144 | bytes 60332316 | solution.py:79
  91.2 16.1 %fusion.196 = (f32[4,512]{1,0:T(4,128)S(1)}, f32[4,512,1536]{2,1,0:T(8,128)}) fusion(f32[4,512,1536]{2,1,0:T(8,128)} %fusion.195, pred[512,1536]{1,0:T(8,128)(4,1)S(1)} %compare_and_fusion.8), kind=kOutput, calls=%fused_computation.224.clone.1 | output fusion | flops 18875904 | bytes 25960448 | tf_op jit(solution)/shard_map/while/body/eval_jaxpr/sub | solution.py:73
  116.8 7.5 fusion.195
  124.3 16.1 %fusion.196 = (f32[4,512]{1,0:T(4,128)S(1)}, f32[4,512,1536]{2,1,0:T(8,128)}) fusion(f32[4,512,1536]{2,1,0:T(8,128)} %fusion.195, pred[512,1536]{1,0:T(8,128)(4,1)S(1)} %compare_and_fusion.8), kind=kOutput, calls=%fused_computation.224.clone.1 | output fusion | flops 18875904 | bytes 25960448 | tf_op jit(solution)/shard_map/while/body/eval_jaxpr/sub | solution.py:73
  149.8 7.5 fusion.195
  157.3 16.1 %fusion.196 = (f32[4,512]{1,0:T(4,128)S(1)}, f32[4,512,1536]{2,1,0:T(8,128)}) fusion(f32[4,512,1536]{2,1,0:T(8,128)} %fusion.195, pred[512,1536]{1,0:T(8,128)(4,1)S(1)} %compare_and_fusion.8), kind=kOutput, calls=%fused_computation.224.clone.1 | output fusion | flops 18875904 | bytes 25960448 | tf_op jit(solution)/shard_map/while/body/eval_jaxpr/sub | solution.py:73
  190.4 16.1 %fusion.196 = (f32[4,512]{1,0:T(4,128)S(1)}, f32[4,512,1536]{2,1,0:T(8,128)}) fusion(f32[4,512,1536]{2,1,0:T(8,128)} %fusion.195, pred[512,1536]{1,0:T(8,128)(4,1)S(1)} %compare_and_fusion.8), kind=kOutput, calls=%fused_computation.224.clone.1 | output fusion | flops 18875904 | bytes 25960448 | tf_op jit(solution)/shard_map/while/body/eval_jaxpr/sub | solution.py:73
  220.1 44.2 %reduce-scatter.6.cloned.1.call-done = bf16[512,1024]{1,0:T(8,128)(2,1)} async-done(((bf16[2048,1024]{1,0:T(8,128)(2,1)}), bf16[512,1024]{1,0:T(8,128)(2,1)}) %reduce-scatter.6.cloned.1.call-update) | async-done | bytes 1048592 | tf_op jit(solution)/shard_map/reduce_scatter | solution.py:196
  268.3 34.6 %all-gather.16.cloned.1.call-done = bf16[2048,1024]{1,0:T(8,128)(2,1)} async-done(((bf16[512,1024]{1,0:T(8,128)(2,1)}), bf16[2048,1024]{1,0:T(8,128)(2,1)}) %all-gather.16.cloned.1.call-update) | async-done | bytes 4194320 | tf_op jit(solution)/shard_map/all_gather | solution.py:205
  302.9 12.9 fusion.81
  315.9 44.7 %reduce-scatter.8.cloned.1.call-done = bf16[512,1024]{1,0:T(8,128)(2,1)} async-done(((bf16[2048,1024]{1,0:T(8,128)(2,1)}), bf16[512,1024]{1,0:T(8,128)(2,1)}) %reduce-scatter.8.cloned.1.call-update) | async-done | bytes 1048592 | tf_op jit(solution)/shard_map/reduce_scatter | solution.py:211
  367.3 34.4 %all-gather.18.cloned.1.call-done = bf16[2048,1024]{1,0:T(8,128)(2,1)} async-done(((bf16[512,1024]{1,0:T(8,128)(2,1)}), bf16[2048,1024]{1,0:T(8,128)(2,1)}) %all-gather.18.cloned.1.call-update) | async-done | bytes 4194320 | tf_op jit(solution)/shard_map/all_gather | solution.py:181
  412.2 59.8 %while.43 = (s32[]{:T(128)}, bf16[4,512,4,64]{1,3,2,0:T(8,128)(2,1)}, f32[4,4,512]{2,1,0:T(4,128)S(1)}, s32[4]{0:T(128)S(1)}, bf16[3072,4,64]{0,2,1:T(8,128)(2,1...) while((s32[]{:T(128)}, ...), condition=%wide.region_17.19_spmd, body=%wide.region_14.18_spmd.sunk | while | flops 845545472 | bytes 43079948 | solution.py:79
  479.2 44.2 %reduce-scatter.10.cloned.1.call-done = bf16[512,1024]{1,0:T(8,128)(2,1)} async-done(((bf16[2048,1024]{1,0:T(8,128)(2,1)}), bf16[512,1024]{1,0:T(8,128)(2,1)}) %reduce-scatter.10.cloned.1.call-update) | async-done | bytes 1048592 | tf_op jit(solution)/shard_map/reduce_scatter | solution.py:196
  528.2 33.8 %all-gather.20.cloned.1.call-done = bf16[2048,1024]{1,0:T(8,128)(2,1)} async-done(((bf16[512,1024]{1,0:T(8,128)(2,1)}), bf16[2048,1024]{1,0:T(8,128)(2,1)}) %all-gather.20.cloned.1.call-update) | async-done | bytes 4194320 | tf_op jit(solution)/shard_map/all_gather | solution.py:205
  562.0 8.9 fusion.146
  570.9 27.1 %all-gather.22.cloned.1.call-done = bf16[2048,1024]{1,0:T(8,128)(2,1)} async-done(((bf16[512,1024]{1,0:T(8,128)(2,1)}), bf16[2048,1024]{1,0:T(8,128)(2,1)}) %all-gather.22.cloned.1.call-update) | async-done | bytes 4194320 | tf_op jit(solution)/shard_map/all_gather | solution.py:254
  598.0 15.4 %fusion.141 = (bf16[1024]{0:T(1024)(128)(2,1)}, bf16[2048,1024]{1,0:T(8,128)(2,1)S(1)}) fusion(f32[2048,1024]{1,0:T(8,128)} %fusion.146, f32[1024]{0:T(1024)S(1)} %copy-done.59, bf16[2048,1024]{1,0:T(8,128)(2,1)} %all-gather.22.cloned.1.call-done, bf16[1024,1024]{1,0:T(8,128)(2,1)} %param.40), kind=kOutput, calls=%fused_computation.222 | convolution fusion | flops 4349492224 | bytes 18880512 | tf_op jit(solution)/shard_map/dot_general | solution.py:45
  622.0 44.5 %reduce-scatter.12.cloned.1.call-done = bf16[512,1024]{1,0:T(8,128)(2,1)} async-done(((bf16[2048,1024]{1,0:T(8,128)(2,1)}), bf16[512,1024]{1,0:T(8,128)(2,1)}) %reduce-scatter.12.cloned.1.call-update) | async-done | bytes 1048592 | tf_op jit(solution)/shard_map/reduce_scatter | solution.py:262
  676.7 34.6 %all-gather.24.cloned.1.call-done = bf16[2048,1024]{1,0:T(8,128)(2,1)} async-done(((bf16[512,1024]{1,0:T(8,128)(2,1)}), bf16[2048,1024]{1,0:T(8,128)(2,1)}) %all-gather.24.cloned.1.call-update) | async-done | bytes 4194320 | tf_op jit(solution)/shard_map/all_gather | solution.py:272
  719.7 133.1 %while.44 = (s32[]{:T(128)}, f32[3072,4,64]{0,2,1:T(8,128)}, f32[3072,4,64]{0,2,1:T(8,128)}, bf16[4,512,4,64]{1,0,3,2:T(4,128)(2,1)}, s32[4]{0:T(128)S(1)}, /*in...) while((s32[]{:T(128)}, f32[3072,4,64]{0,2,1:T(8,128)}, ...), condition=%wide.region_26.28_spmd, body=%wide.region_24.27_spmd.sunk | while | flops 2045378560 | bytes 146864608 | solution.py:133
  855.8 9.5 convolution_convert_fusion.4
  865.3 11.0 fusion.110
  896.5 22.6 %all-reduce.5 = (bf16[2,3,64]{2,1,0:T(4,128)(2,1)S(1)}, bf16[1024]{0:T(1024)(128)(2,1)S(1)}) all-reduce(bf16[2,3,64]{2,1,0:T(4,128)(2,1)S(1)} %pad_maximum_fusion.2, bf16[1024]{0:T(1024)(128)(2,1)S(1)} %copy-done.52), channel_id=1, replica_groups=mesh['dp'=8,'mp'=4] {'dp'}, use_global_device_ids=true, to_apply=%region_38.40 | all-reduce | flops 1408 | bytes 5632 | tf_op jit(solution)/shard_map/psum | solution.py:317
  923.4 129.8 %all-reduce.9.cloned.1.call-done = (bf16[2,2,64,1024]{3,2,1,0:T(8,128)(2,1)}, bf16[1024,1024]{1,0:T(8,128)(2,1)}, bf16[1024,1024]{1,0:T(8,128)(2,1)}) async-done(((bf16[2,2,64,1024]{3,2,1,0:T(8,128)(2,1)}, bf16[1024,1024]{1,0:T(8,128)(2,1)}, bf16[1024,1024]{1,0:T(8,128)(2,1)}), (bf16[2,2,64,1024]{3,2,1,0:T(8,128)(2,1)}, bf16[1024,1024]{1,0:T(8,128)(2,1)}, ...) | async-done | bytes 4718608 | tf_op jit(solution)/shard_map/psum | solution.py:318
  1062.0 37.1 %reduce-scatter.14.cloned.1.call-done = bf16[512,1024]{1,0:T(8,128)(2,1)} async-done(((bf16[2048,1024]{1,0:T(8,128)(2,1)}), bf16[512,1024]{1,0:T(8,128)(2,1)}) %reduce-scatter.14.cloned.1.call-update) | async-done | bytes 1048592 | tf_op jit(solution)/shard_map/reduce_scatter | solution.py:297
  1103.5 44.4 %all-reduce.4 = (f32[1024]{0:T(1024)}, f32[1024]{0:T(1024)}, f32[1024]{0:T(1024)}, f32[1024]{0:T(1024)}, f32[1024]{0:T(1024)}, /*index=5*/f32[1024]{0:T(1024)}) all-reduce(f32[1024]{0:T(1024)S(1)} %get-tuple-element.386, f32[1024]{0:T(1024)S(1)} %get-tuple-element.390, ...), channel_id=1, replica_groups=mesh['dp'=8,'mp'=4] {'dp','mp'}, use_global_device_ids=true, to_apply=%region_32.34 | all-reduce | flops 6144 | bytes 49152 | tf_op jit(solution)/shard_map/psum | solution.py:323
  1150.8 101.9 %all-gather.28.cloned.1.call-done = bf16[8192,2,5,64]{0,3,2,1:T(8,128)(2,1)} async-done(((bf16[1024,2,5,64]{0,3,2,1:T(8,128)(2,1)}), bf16[8192,2,5,64]{0,3,2,1:T(8,128)(2,1)}) %all-gather.28.cloned.1.call-update) | async-done | bytes 10485776 | tf_op jit(solution)/shard_map/all_gather | solution.py:314
  1252.7 20.2 %copy.76 = bf16[80,8,8,1024]{3,2,1,0:T(8,128)(2,1)} copy(bf16[80,8,8,1024]{3,1,2,0:T(8,128)(2,1)} %bitcast.173) | data formatting | bytes 20971520
  1272.9 13.1 %reduce_sum.314 = bf16[1024,2,5,64]{0,3,2,1:T(8,128)(2,1)S(1)} reduce(bf16[8,1024,2,5,64]{1,0,4,3,2:T(8,128)(2,1)} %bitcast.171, bf16[]{:T(256)} %constant.219.clone.1), dimensions={0}, to_apply=%region_35.37 | reduce | flops 4587520 | bytes 11796482 | tf_op jit(solution)/shard_map/reduce_sum | solution.py:314
  (404 shorter events, 360.2 us)
Async XLA Ops:
  7.2 295.7 %copy-start = (bf16[1024,1024]{1,0:T(8,128)(2,1)S(1)}, bf16[1024,1024]{1,0:T(8,128)(2,1)}, u32[]{:S(2)}) copy-start(bf16[1024,1024]{1,0:T(8,128)(2,1)} %param.38) | copy-start | bytes 6291460
  7.2 27.7 %all-gather.14.cloned.1.call-start = ((), (), s32[]{:S(2)}) async-start(), calls=%async_computation.6 | async-start | bytes 2621440 | tf_op jit(solution)/shard_map/all_gather | solution.py:172
  8.0 63.5 %all-gather.12.cloned.1.call-start = ((), (), s32[]{:S(2)}) async-start(), calls=%async_computation.5 | async-start | bytes 5242880 | tf_op jit(solution)/shard_map/all_gather | solution.py:181
  12.8 251.5 %reduce-scatter.6.cloned.1.call-start = ((), (), s32[]{:S(2)}) async-start(), calls=%async_computation.7 | async-start | bytes 5242880 | tf_op jit(solution)/shard_map/reduce_scatter | solution.py:196
  13.0 63.9 %copy-start.38 = (f32[2,2,64]{2,1,0:T(2,128)}, f32[2,2,64]{2,1,0:T(2,128)S(1)}, u32[]{:S(2)}) copy-start(f32[2,2,64]{2,1,0:T(2,128)S(1)} %copy.44) | copy-start | bytes 3076
  13.3 63.5 %copy-start.48 = (f32[2,64]{1,0:T(2,128)}, f32[2,64]{1,0:T(2,128)S(1)}, u32[]{:S(2)}) copy-start(f32[2,64]{1,0:T(2,128)S(1)} %slice_bitcast_fusion) | copy-start | bytes 1540
  219.6 44.8 %copy-start.4 = (bf16[512,1024]{1,0:T(8,128)(2,1)S(1)}, bf16[512,1024]{1,0:T(8,128)(2,1)}, u32[]{:S(2)}) copy-start(bf16[512,1024]{1,0:T(8,128)(2,1)} %param.25) | copy-start | bytes 3145732
  219.6 44.8 %copy-start.26 = (f32[1024]{0:T(1024)S(1)}, f32[1024]{0:T(1024)}, u32[]{:S(2)}) copy-start(f32[1024]{0:T(1024)} %param.35) | copy-start | bytes 12292
  219.6 47.1 %copy-start.27 = (f32[1024]{0:T(1024)S(1)}, f32[1024]{0:T(1024)}, u32[]{:S(2)}) copy-start(f32[1024]{0:T(1024)} %param.36) | copy-start | bytes 12292
  219.6 47.1 %copy-start.42 = (f32[1024]{0:T(1024)S(1)}, f32[1024]{0:T(1024)}, u32[]{:S(2)}) copy-start(f32[1024]{0:T(1024)} %param.37) | copy-start | bytes 12292
  219.6 83.3 %all-gather.16.cloned.1.call-start = ((), (), s32[]{:S(2)}) async-start(), calls=%async_computation.8 | async-start | bytes 5242880 | tf_op jit(solution)/shard_map/all_gather | solution.py:205
  268.3 92.3 %reduce-scatter.8.cloned.1.call-start = ((), (), s32[]{:S(2)}) async-start(), calls=%async_computation.9 | async-start | bytes 5242880 | tf_op jit(solution)/shard_map/reduce_scatter | solution.py:211
  315.8 44.8 %copy-start.51 = (f32[1024]{0:T(1024)S(1)}, f32[1024]{0:T(1024)}, u32[]{:S(2)}) copy-start(f32[1024]{0:T(1024)} %param.41) | copy-start | bytes 12292
  315.9 49.7 %copy-start.30 = (f32[1024]{0:T(1024)S(1)}, f32[1024]{0:T(1024)}, u32[]{:S(2)}) copy-start(f32[1024]{0:T(1024)} %param.30) | copy-start | bytes 12292
  315.9 49.7 %copy-start.41 = (f32[1024]{0:T(1024)S(1)}, f32[1024]{0:T(1024)}, u32[]{:S(2)}) copy-start(f32[1024]{0:T(1024)} %param.31) | copy-start | bytes 12292
  315.9 85.8 %all-gather.18.cloned.1.call-start = ((), (), s32[]{:S(2)}) async-start(), calls=%async_computation.10 | async-start | bytes 5242880 | tf_op jit(solution)/shard_map/all_gather | solution.py:181
  367.0 156.4 %reduce-scatter.10.cloned.1.call-start = ((), (), s32[]{:S(2)}) async-start(), calls=%async_computation.11 | async-start | bytes 5242880 | tf_op jit(solution)/shard_map/reduce_scatter | solution.py:196
  478.7 47.1 %copy-start.28 = (f32[1024]{0:T(1024)S(1)}, f32[1024]{0:T(1024)}, u32[]{:S(2)}) copy-start(f32[1024]{0:T(1024)} %param.36) | copy-start | bytes 12292
  478.7 47.0 %copy-start.43 = (f32[1024]{0:T(1024)S(1)}, f32[1024]{0:T(1024)}, u32[]{:S(2)}) copy-start(f32[1024]{0:T(1024)} %param.37) | copy-start | bytes 12292
  478.7 83.3 %all-gather.20.cloned.1.call-start = ((), (), s32[]{:S(2)}) async-start(), calls=%async_computation.12 | async-start | bytes 5242880 | tf_op jit(solution)/shard_map/all_gather | solution.py:205
  527.4 70.7 %all-gather.22.cloned.1.call-start = ((), (), s32[]{:S(2)}) async-start(), calls=%async_computation.13 | async-start | bytes 5242880 | tf_op jit(solution)/shard_map/all_gather | solution.py:254
  528.1 69.9 %copy-start.59 = (f32[1024]{0:T(1024)S(1)}, f32[1024]{0:T(1024)}, u32[]{:S(2)}) copy-start(f32[1024]{0:T(1024)} %param.39) | copy-start | bytes 12292
  528.1 138.4 %reduce-scatter.12.cloned.1.call-start = ((), (), s32[]{:S(2)}) async-start(), calls=%async_computation.14 | async-start | bytes 5242880 | tf_op jit(solution)/shard_map/reduce_scatter | solution.py:262
  621.8 44.8 %copy-start.8 = (bf16[512,1024]{1,0:T(8,128)(2,1)S(1)}, bf16[512,1024]{1,0:T(8,128)(2,1)}, u32[]{:S(2)}) copy-start(bf16[512,1024]{1,0:T(8,128)(2,1)} %reduce-scatter.10.cloned.1.call-done) | copy-start | bytes 3145732
  621.8 89.5 %all-gather.24.cloned.1.call-start = ((), (), s32[]{:S(2)}) async-start(), calls=%async_computation.15 | async-start | bytes 5242880 | tf_op jit(solution)/shard_map/all_gather | solution.py:272
  676.6 243.6 %all-gather.26.cloned.1.call-start = ((), (), s32[]{:S(2)}) async-start(), calls=%async_computation.17 | async-start | bytes 2621440 | tf_op jit(solution)/shard_map/all_gather | solution.py:306
  855.5 197.6 %all-reduce.9.cloned.1.call-start = ((), (), s32[]{:S(2)}) async-start(), calls=%async_computation.19 | async-start | bytes 9437184 | tf_op jit(solution)/shard_map/psum | solution.py:318
  878.4 220.7 %reduce-scatter.14.cloned.1.call-start = ((), (), s32[]{:S(2)}) async-start(), calls=%async_computation.16 | async-start | bytes 5242880 | tf_op jit(solution)/shard_map/reduce_scatter | solution.py:297
  889.5 363.2 %all-gather.28.cloned.1.call-start = ((), (), s32[]{:S(2)}) async-start(), calls=%async_computation.18 | async-start | bytes 11796480 | tf_op jit(solution)/shard_map/all_gather | solution.py:314
  1059.5 41.6 %copy-start.37 = (f32[512]{0:T(512)S(1)}, f32[512]{0:T(512)}, u32[]{:S(2)}) copy-start(f32[512]{0:T(512)} %copy-done.36) | copy-start | bytes 6148
  1059.5 41.6 %copy-start.35 = (f32[512]{0:T(512)S(1)}, f32[512]{0:T(512)}, u32[]{:S(2)}) copy-start(f32[512]{0:T(512)} %copy-done.34) | copy-start | bytes 6148
  1062.0 85.9 %copy-start.10 = (f32[512,1024]{1,0:T(8,128)S(1)}, f32[512,1024]{1,0:T(8,128)}, u32[]{:S(2)}) copy-start(f32[512,1024]{1,0:T(8,128)} %copy-done.9) | copy-start | bytes 6291460
  (62 other events, 680.7 us)
Sparse Core Ops, SparseCore 0:
  9.6 25.2 all-gather.13
  37.1 34.4 all-gather.11
  219.7 44.5 reduce-scatter.5
  268.4 34.4 all-gather.15
  316.0 44.5 reduce-scatter.7
  367.2 34.4 all-gather.17
  478.8 44.5 reduce-scatter.9
  527.5 34.4 all-gather.19
  563.6 34.4 all-gather.21
  621.9 44.5 reduce-scatter.11
  676.8 34.4 all-gather.23
  855.6 22.5 all-gather.25
  883.3 169.7 all-reduce.8
  1055.5 43.5 reduce-scatter.13
  1101.2 151.4 all-gather.27
